TPU v7x, 32 devices: a whole 2x2x4 slice. The times are simulated.
32 devices in a mesh: ep: 16 (over z, y, core), dp: 2 (over x).
Axes of the slice: x: 2, y: 2, z: 4, core: 2. Of those that a mesh axis runs over, the one named last changes fastest.
Arguments:
- tokens: bfloat16 [512, 3584], P(('ep', 'dp')), may hold values from -6 to 6
- norm_gain: float32 [3584], replicated, may hold values from 0.25 to 1.75
- router: bfloat16 [3584, 16], replicated, may hold values from -0.09375 to 0.09375
- next_router: bfloat16 [3584, 16], P('dp'), may hold values from -0.09375 to 0.09375
- expert_ids: int32 [512, 8], P(('ep', 'dp')), may hold values from 0 to 15, all different within a row; in each aligned block of 16 rows (0 to 15, 16 to 31, ...) at most 16 rows name the same one
- store: bfloat16 [16, 2, 224, 128, 128], P('ep', 'dp'), may hold values from -0.125 to 0.125
- send_list: int32 [16, 224], P('ep'), may hold values from -1 to 223, as said below
- cache_map: int32 [16, 224], P('ep'), may hold values from 0 to 223, as said below
Outputs:
- layer_out: bfloat16 [512, 3584], P(('ep', 'dp'))
- next_scores: float32 [512, 16], P(('ep', 'dp'))
Inputs may be any that keep to these rules, and one draw needn't show every extreme that they name: `expert_ids`: each row names 8 different experts; among the rows of one device no expert is named by more than 16 rows, a bound that some block reaches. `send_list`: an entry is -1 where that arriving slot stays empty; every row names each of the 224 store indices exactly once. `cache_map`: each entry numbers an arriving slot of that device that is never empty; the entries of a row are distinct.
All inputs are finite; a program needn't handle non-finite values.
Results may differ from a plain program's by a relative error of at most 0.0095.
Values may be sent and summed in bfloat16 or wider, within the bound.
No kernel may reach another device: no remote copies, remote signals or barrier semaphores. Data moves between devices by JAX's collectives and lax.ppermute only.
A program may use at most 64 MiB of HBM per device.

v0:
```python
import jax
import jax.numpy as jnp
from jax import lax
from jax.sharding import PartitionSpec as P


def per_device(tokens, norm_gain, router, next_router, expert_ids, store, send_list, cache_map):
    tok_dev, width = tokens.shape
    n_dp = lax.axis_size("dp")
    experts = router.shape[1]
    top = expert_ids.shape[1]
    tiles = cache_map.shape[1]
    tile_rows = store.shape[3]
    tile_cols = store.shape[4]
    part = width // n_dp
    row_tiles = part // tile_rows
    col_tiles = tiles // (2 * row_tiles)
    hidden_width = col_tiles * tile_cols
    capacity = min(tok_dev, max(2, 2 * tok_dev * top // experts))
    values = tokens.astype(jnp.float32)
    scale = lax.rsqrt(jnp.mean(values * values, axis=1, keepdims=True) + 1e-06)
    normed = (values * scale * norm_gain).astype(jnp.bfloat16)
    scores = jax.nn.sigmoid(jnp.dot(normed, router, preferred_element_type=jnp.float32))
    chosen = (expert_ids[:, :, None] == jnp.arange(experts, dtype=jnp.int32)[None, None, :]).astype(
        jnp.float32
    )
    picked = jnp.sum(chosen * scores[:, None, :], axis=2)
    weights = (2.5 * picked / jnp.sum(picked, axis=1, keepdims=True)).astype(jnp.bfloat16)
    flat = chosen.reshape(tok_dev * top, experts)
    before = jnp.cumsum(flat, axis=0) - flat
    rank = jnp.sum(before * flat, axis=1).astype(jnp.int32)
    slot = expert_ids.reshape(-1) * capacity + rank
    columns = jnp.arange(experts * capacity, dtype=jnp.int32)
    match = (slot[:, None] == columns[None, :]).reshape(tok_dev, top, experts * capacity)
    dispatch = jnp.sum(match.astype(jnp.float32), axis=1).astype(jnp.bfloat16)
    combine = jnp.sum(
        jnp.where(match, weights.astype(jnp.float32)[:, :, None], 0.0), axis=1
    ).astype(jnp.bfloat16)
    outgoing = lax.dot_general(
        dispatch, normed, (((0,), (0,)), ((), ())), preferred_element_type=jnp.float32
    ).astype(jnp.bfloat16)
    owned = store.reshape(tiles, tile_rows, tile_cols)
    wanted = send_list.reshape(-1)
    present = wanted >= 0
    leaving = jnp.where(
        present[:, None, None], owned[jnp.maximum(wanted, 0)], jnp.zeros((), jnp.bfloat16)
    )
    arrived = lax.all_to_all(leaving, "ep", split_axis=0, concat_axis=0, tiled=True)
    cached = arrived[cache_map.reshape(-1)].reshape(2, row_tiles, col_tiles, tile_rows, tile_cols)
    up_tiles = cached[0]
    down_tiles = cached[1]
    rows = lax.all_to_all(
        lax.all_to_all(outgoing, "ep", split_axis=0, concat_axis=0, tiled=True),
        "dp",
        split_axis=1,
        concat_axis=0,
        tiled=True,
    )
    count = rows.shape[0]
    block = rows.reshape(count, row_tiles, tile_rows)
    product = jnp.einsum("nat,acts->ncs", block, up_tiles, preferred_element_type=jnp.float32)
    summed = lax.psum(product.reshape(count, hidden_width).astype(jnp.bfloat16), "dp").astype(
        jnp.float32
    )
    hidden = jax.nn.silu(summed).astype(jnp.bfloat16)
    number = hidden.shape[0]
    product = jnp.einsum(
        "ncs,acts->nat",
        hidden.reshape(number, col_tiles, tile_cols),
        down_tiles,
        preferred_element_type=jnp.float32,
    )
    result = product.reshape(number, part).astype(jnp.bfloat16)
    back = lax.all_to_all(
        lax.all_to_all(result, "dp", split_axis=0, concat_axis=1, tiled=True),
        "ep",
        split_axis=0,
        concat_axis=0,
        tiled=True,
    )
    mixed = jnp.dot(combine, back, preferred_element_type=jnp.float32)
    layer_out = (values + mixed).astype(jnp.bfloat16)
    stream = layer_out.astype(jnp.float32)
    renorm = lax.rsqrt(jnp.mean(stream * stream, axis=1, keepdims=True) + 1e-06)
    next_normed = (stream * renorm).astype(jnp.bfloat16)
    features = lax.all_to_all(next_normed, "dp", split_axis=1, concat_axis=0, tiled=True)
    partial_scores = jnp.dot(features, next_router, preferred_element_type=jnp.float32)
    next_logits = lax.psum_scatter(
        partial_scores.astype(jnp.bfloat16), "dp", scatter_dimension=0, tiled=True
    ).astype(jnp.float32)
    return (layer_out, jax.nn.sigmoid(next_logits))


def solution(mesh):
    in_specs = (
        P(("ep", "dp"), None),
        P(),
        P(),
        P("dp", None),
        P(("ep", "dp"), None),
        P("ep", "dp", None, None, None),
        P("ep", None),
        P("ep", None),
    )
    out_specs = (P(("ep", "dp"), None), P(("ep", "dp"), None))
    return jax.shard_map(
        per_device, mesh=mesh, in_specs=in_specs, out_specs=out_specs, check_vma=False
    )
```

profile of v0, /device:TPU:0, one launch (start us, length us, event | category | flops | bytes accessed | tf_op | source)
XLA Modules:
  0.0 437.3 jit_solution(8908242254397563168)
XLA Ops:
  7.2 0.0 copy-start
  7.2 0.0 copy-start.6
  7.2 1.1 fusion.17
  8.3 0.8 copy.46
  9.0 0.1 eq.36
  9.1 0.0 copy-done
  9.1 1.1 fusion.11
  10.3 0.3 select_reduce_fusion.1
  10.6 0.1 fusion.20
  10.7 0.2 reduce_window_sum.11
  10.9 0.2 select_reduce_fusion.3
  11.0 0.1 convert_element_type.76
  11.1 0.1 fusion.25
  11.2 0.2 select_reduce_fusion
  11.4 2.9 convolution_convert_fusion
  14.3 7.4 %all-to-all-start = ((bf16[16,16,3584]{2,1,0:T(8,128)(2,1)}), bf16[16,16,3584]{2,1,0:T(8,128)(2,1)S(1)}, u32[]{:S(2)}, u32[]{:S(2)}) async-start(bf16[16,16,3584]{2,1,0:T(8,128)(2,1)} %bitcast.49), calls=%async_computation | async-start | bytes 3670016 | tf_op jit(solution)/shard_map/all_to_all | solution.py:53
  21.7 0.0 copy-done.6
  21.8 11.5 %gather_fusion = bf16[224,128,128]{2,1,0:T(8,128)(2,1)} fusion(bf16[224,128,128]{2,1,0:T(8,128)(2,1)} %bitcast.50, s32[1024]{0:T(1024)S(1)} %pad_clamp_fusion.1), kind=kCustom, calls=%fused_computation | custom fusion | bytes 14680960 | tf_op jit(solution)/shard_map/gather | solution.py:46
  33.2 24.9 %all-to-all-done = bf16[16,16,3584]{2,1,0:T(8,128)(2,1)S(1)} async-done(((bf16[16,16,3584]{2,1,0:T(8,128)(2,1)}), bf16[16,16,3584]{2,1,0:T(8,128)(2,1)S(1)}, u32[]{:S(2)}, u32[]{:S(2)}) %all-to-all-start) | async-done | bytes 1835040 | tf_op jit(solution)/shard_map/all_to_all | solution.py:53
  58.1 1.5 all_to_all.57
  59.6 3.0 copy.49
  62.6 3.7 all-to-all-start.1
  66.3 6.6 %broadcast_select_fusion = bf16[224,128,128]{2,1,0:T(8,128)(2,1)} fusion(bf16[224,128,128]{2,1,0:T(8,128)(2,1)} %gather_fusion, pred[224]{0:T(512)(128)(4,1)S(1)} %compare_reduce_fusion), kind=kLoop, calls=%fused_computation.2 | loop fusion | flops 3670016 | bytes 14680288 | tf_op jit(solution)/shard_map/jit(_where)/select_n | solution.py:45
  73.0 0.0 copy-start.7
  73.0 16.8 %all-to-all-done.1 = bf16[256,2,1792]{2,0,1:T(8,128)(2,1)S(1)} async-done(((bf16[256,2,1792]{2,0,1:T(8,128)(2,1)}), bf16[256,2,1792]{2,0,1:T(8,128)(2,1)S(1)}, u32[]{:S(2)}, u32[]{:S(2)}) %all-to-all-start.1) | async-done | bytes 1835040 | tf_op jit(solution)/shard_map/all_to_all | solution.py:52
  89.7 9.6 %all-to-all-start.2 = ((bf16[224,128,128]{2,1,0:T(8,128)(2,1)}), bf16[224,128,128]{2,1,0:T(8,128)(2,1)}, u32[]{:S(2)}, u32[]{:S(2)}) async-start(bf16[224,128,128]{2,1,0:T(8,128)(2,1)} %broadcast_select_fusion), calls=%async_computation.2 | async-start | bytes 14680064 | tf_op jit(solution)/shard_map/all_to_all | solution.py:48
  99.4 0.2 all-reduce.2.cloned.1.call-start
  99.6 0.0 copy-done.7
  99.6 2.4 reshape.175
  102.1 129.6 %all-to-all-done.2 = bf16[224,128,128]{2,1,0:T(8,128)(2,1)} async-done(((bf16[224,128,128]{2,1,0:T(8,128)(2,1)}), bf16[224,128,128]{2,1,0:T(8,128)(2,1)}, u32[]{:S(2)}, u32[]{:S(2)}) %all-to-all-start.2) | async-done | bytes 7340064 | tf_op jit(solution)/shard_map/all_to_all | solution.py:48
  231.7 11.4 %gather_fusion.1 = bf16[224,128,128]{2,1,0:T(8,128)(2,1)} fusion(bf16[224,128,128]{2,1,0:T(8,128)(2,1)} %all-to-all-done.2, s32[1024]{0:T(1024)S(1)} %pad_clamp_fusion), kind=kCustom, calls=%fused_computation.1 | custom fusion | bytes 14680960 | tf_op jit(solution)/shard_map/gather | solution.py:49
  243.1 9.4 %fusion.26 = (bf16[112,128,128]{2,1,0:T(8,128)(2,1)}, bf16[112,128,128]{2,1,0:T(8,128)(2,1)}) fusion(bf16[224,128,128]{2,1,0:T(8,128)(2,1)} %gather_fusion.1), kind=kLoop, calls=%fused_computation.56 | loop fusion | bytes 14680064 | tf_op jit(solution)/shard_map/slice | solution.py:50
  252.5 0.0 copy-start.2
  252.5 6.1 %copy.51 = bf16[14,8,128,128]{2,3,1,0:T(8,128)(2,1)} copy(bf16[14,8,128,128]{3,2,1,0:T(8,128)(2,1)} %bitcast.45) | data formatting | bytes 7340032 | tf_op jit(solution)/shard_map/squeeze | solution.py:50
  258.6 0.0 copy-done.2
  258.6 5.1 %bitcast_convert_fusion.1 = bf16[512,1024]{1,0:T(8,128)(2,1)} fusion(bf16[1024,14,128]{2,0,1:T(8,128)(2,1)} %bitcast.52, bf16[512,14,128]{2,1,0:T(8,128)(2,1)S(1)} %copy-done.2), kind=kOutput, calls=%fused_computation.13 | convolution fusion | flops 1879572480 | bytes 6553600 | tf_op jit(solution)/shard_map/nat,acts->ncs/dot_general | solution.py:61
  263.7 0.0 all-reduce.2.cloned.1.call-update
  263.7 0.0 reduce-scatter.2.cloned.1.call-start
  263.7 4.3 copy.53
  268.1 62.6 %all-reduce.2.cloned.1.call-done = bf16[512,1024]{1,0:T(8,128)(2,1)} async-done(((bf16[512,1024]{1,0:T(8,128)(2,1)}), bf16[512,1024]{1,0:T(8,128)(2,1)}) %all-reduce.2.cloned.1.call-update) | async-done | bytes 1048592 | tf_op jit(solution)/shard_map/psum | solution.py:62
  330.6 4.7 %bitcast_convert_fusion = bf16[512,1792]{1,0:T(8,128)(2,1)S(1)} fusion(bf16[1792,8,128]{2,0,1:T(8,128)(2,1)} %bitcast.51, bf16[512,1024]{1,0:T(8,128)(2,1)} %all-reduce.2.cloned.1.call-done), kind=kOutput, calls=%fused_computation.6 | convolution fusion | flops 1883111424 | bytes 6553600 | tf_op jit(solution)/shard_map/ncs,acts->nat/dot_general | solution.py:67
  335.4 24.7 %all_to_all.77 = bf16[2,256,1792]{2,1,0:T(8,128)(2,1)S(1)} all-to-all(bf16[2,256,1792]{2,1,0:T(8,128)(2,1)S(1)} %bitcast.53), channel_id=1, replica_groups=mesh['ep'=16,'dp'=2] {'dp'}, dimensions={0} | all-to-all | bytes 3670016 | tf_op jit(solution)/shard_map/all_to_all | solution.py:75
  360.0 1.9 copy.55
  361.9 0.0 copy-start.3
  361.9 0.0 copy-start.1
  362.0 2.2 all_to_all.64
  364.1 0.0 copy-start.5
  364.1 48.3 %all_to_all.78 = bf16[16,16,3584]{2,1,0:T(8,128)(2,1)S(1)} all-to-all(bf16[16,16,3584]{2,1,0:T(8,128)(2,1)} %all_to_all.64), channel_id=1, replica_groups=mesh['ep'=16,'dp'=2] {'ep'}, dimensions={0} | all-to-all | bytes 3670016 | tf_op jit(solution)/shard_map/all_to_all | solution.py:74
  412.5 0.0 copy-done.3
  412.5 0.5 fusion.15
  412.9 0.0 copy-start.4
  413.0 0.1 fusion.16
  413.1 7.3 %all_to_all.79 = bf16[16,2,1792]{2,0,1:T(8,128)(2,1)S(1)} all-to-all(bf16[16,2,1792]{2,0,1:T(8,128)(2,1)S(1)} %bitcast.55), channel_id=1, replica_groups=mesh['ep'=16,'dp'=2] {'dp'}, dimensions={1} | all-to-all | bytes 229376 | tf_op jit(solution)/shard_map/all_to_all | solution.py:86
  420.4 0.0 copy-done.5
  420.4 0.8 convolution_convert_fusion.1
  421.1 0.0 reduce-scatter.2.cloned.1.call-update
  421.2 8.0 %reduce-scatter.2.cloned.1.call-done = bf16[16,16]{1,0:T(8,128)(2,1)} async-done(((bf16[32,16]{1,0:T(8,128)(2,1)}), bf16[16,16]{1,0:T(8,128)(2,1)}) %reduce-scatter.2.cloned.1.call-update) | async-done | bytes 528 | tf_op jit(solution)/shard_map/reduce_scatter | solution.py:88
  429.2 1.3 add_divide_fusion
  430.5 0.0 copy-done.4
  430.5 0.0 copy-done.1
  (10 shorter events, 0.1 us)
Async XLA Ops:
  7.2 2.0 copy-start
  7.2 14.5 %copy-start.6 = (s32[1,224]{1,0:T(1,128)S(1)}, s32[1,224]{1,0:T(1,128)}, u32[]{:S(2)}) copy-start(s32[1,224]{1,0:T(1,128)} %param.14) | copy-start | bytes 2692
  14.3 43.8 %all-to-all-start = ((bf16[16,16,3584]{2,1,0:T(8,128)(2,1)}), bf16[16,16,3584]{2,1,0:T(8,128)(2,1)S(1)}, u32[]{:S(2)}, u32[]{:S(2)}) async-start(bf16[16,16,3584]{2,1,0:T(8,128)(2,1)} %bitcast.49), calls=%async_computation | async-start | bytes 3670016 | tf_op jit(solution)/shard_map/all_to_all | solution.py:53
  62.6 27.1 %all-to-all-start.1 = ((bf16[256,2,1792]{2,0,1:T(8,128)(2,1)}), bf16[256,2,1792]{2,0,1:T(8,128)(2,1)S(1)}, u32[]{:S(2)}, u32[]{:S(2)}) async-start(bf16[256,2,1792]{2,0,1:T(8,128)(2,1)} %copy.49), calls=%async_computation.1 | async-start | bytes 3670016 | tf_op jit(solution)/shard_map/all_to_all | solution.py:52
  73.0 26.7 %copy-start.7 = (s32[1,224]{1,0:T(1,128)S(1)}, s32[1,224]{1,0:T(1,128)}, u32[]{:S(2)}) copy-start(s32[1,224]{1,0:T(1,128)} %param.15) | copy-start | bytes 2692
  89.7 142.0 %all-to-all-start.2 = ((bf16[224,128,128]{2,1,0:T(8,128)(2,1)}), bf16[224,128,128]{2,1,0:T(8,128)(2,1)}, u32[]{:S(2)}, u32[]{:S(2)}) async-start(bf16[224,128,128]{2,1,0:T(8,128)(2,1)} %broadcast_select_fusion), calls=%async_computation.2 | async-start | bytes 14680064 | tf_op jit(solution)/shard_map/all_to_all | solution.py:48
  99.4 231.3 %all-reduce.2.cloned.1.call-start = ((), (), s32[]{:S(2)}) async-start(), calls=%async_computation.7 | async-start | bytes 2097152 | tf_op jit(solution)/shard_map/psum | solution.py:62
  252.5 6.1 %copy-start.2 = (bf16[512,14,128]{2,1,0:T(8,128)(2,1)S(1)}, bf16[512,14,128]{2,1,0:T(8,128)(2,1)}, u32[]{:S(2)}) copy-start(bf16[512,14,128]{2,1,0:T(8,128)(2,1)} %reshape.175) | copy-start | bytes 5505028
  263.7 165.5 %reduce-scatter.2.cloned.1.call-start = ((), (), s32[]{:S(2)}) async-start(), calls=%async_computation.8 | async-start | bytes 12288 | tf_op jit(solution)/shard_map/reduce_scatter | solution.py:88
  361.9 50.5 %copy-start.3 = (bf16[16,3584]{1,0:T(8,128)(2,1)S(1)}, bf16[16,3584]{1,0:T(8,128)(2,1)}, u32[]{:S(2)}) copy-start(bf16[16,3584]{1,0:T(8,128)(2,1)} %param.8) | copy-start | bytes 344068
  361.9 68.5 %copy-start.1 = (bf16[3584,16]{0,1:T(8,128)(2,1)S(1)}, bf16[3584,16]{0,1:T(8,128)(2,1)}, u32[]{:S(2)}) copy-start(bf16[3584,16]{0,1:T(8,128)(2,1)} %param.10) | copy-start | bytes 344068
  364.1 56.3 %copy-start.5 = (bf16[1792,16]{0,1:T(8,128)(2,1)S(1)}, bf16[1792,16]{0,1:T(8,128)(2,1)}, u32[]{:S(2)}) copy-start(bf16[1792,16]{0,1:T(8,128)(2,1)} %param.11) | copy-start | bytes 172036
  412.9 17.5 %copy-start.4 = (bf16[16,3584]{1,0:T(8,128)(2,1)}, bf16[16,3584]{1,0:T(8,128)(2,1)S(1)}, u32[]{:S(2)}) copy-start(bf16[16,3584]{1,0:T(8,128)(2,1)S(1)} %get-tuple-element.9) | copy-start | bytes 344068
Sparse Core Ops, SparseCore 0:
  263.8 66.7 all-reduce.1
  421.3 7.8 reduce-scatter.1
where the time goes:
time: 438 us; the launch traced here: 437 us
  waiting for transfers between devices  242 us (55%)
  blocking collectives  80.3 us (18%)
  local copies, waits for them, and re-layouts  54.6 us (12%)
  starting transfers between devices  21 us (5%)
  matrix products  15.1 us (3%)
  between operations  14.2 us (3%)
  other arithmetic  10.1 us (2%)
    all_to_all x1, waiting for transfers between devices, per_device(): lax.all_to_all(leaving, 'ep', split_axis=0, concat_axis=0, tiled=True)  130 us
    psum x1, waiting for transfers between devices, per_device(): lax.psum(product.reshape(count, hidden_width).astype(jnp.bfloat16), 'dp')  62.6 us
    all_to_all x1, blocking collectives, per_device(): lax.all_to_all(lax.all_to_all(result, 'dp', split_axis=0, concat_axis=1,...  48.3 us
    all_to_all x1, waiting for transfers between devices, per_device(): lax.all_to_all(outgoing, 'ep', split_axis=0, concat_axis=0, tiled=True)  24.9 us
    all_to_all x1, blocking collectives, per_device(): lax.all_to_all(result, 'dp', split_axis=0, concat_axis=1, tiled=True)  24.7 us
    all_to_all x1, waiting for transfers between devices, per_device(): lax.all_to_all(lax.all_to_all(outgoing, 'ep', split_axis=0, concat_axis=0...  16.8 us
    gather x1, local copies, waits for them, and re-layouts, per_device(): owned[jnp.maximum(wanted, 0)]  11.5 us
    gather x1, local copies, waits for them, and re-layouts, per_device(): arrived[cache_map.reshape(-1)]  11.4 us
  transfers between devices with their start and end apart: 5, of which 5 were waited for; matrix products, arithmetic and copies ran while one was open for 6% of the time, Pallas kernels for 0%

commit v1 on v0

--- a/solution.py
+++ b/solution.py
@@ -59,9 +59,9 @@
     count = rows.shape[0]
     block = rows.reshape(count, row_tiles, tile_rows)
     product = jnp.einsum("nat,acts->ncs", block, up_tiles, preferred_element_type=jnp.float32)
-    summed = lax.psum(product.reshape(count, hidden_width).astype(jnp.bfloat16), "dp").astype(
-        jnp.float32
-    )
+    summed = jnp.sum(
+        lax.all_gather(product.reshape(count, hidden_width).astype(jnp.bfloat16), "dp"), axis=0
+    ).astype(jnp.float32)
     hidden = jax.nn.silu(summed).astype(jnp.bfloat16)
     number = hidden.shape[0]
     product = jnp.einsum(

time: 438 us -> 434 us (level)
  waiting for transfers between devices: 242 us -> 235 us
    psum x1 -> x0, waiting for transfers between devices: 62.6 us -> none  [per_device(): lax.psum(product.reshape(count, hidden_width).astype(jnp.bfloat16), 'dp')]
    all_gather x0 -> x1, waiting for transfers between devices: none -> 55.6 us  [per_device(): lax.all_gather(product.reshape(count, hidden_width).astype(jnp.bfloat16),...]
where the time goes in v1:
time: 434 us; the launch traced here: 433 us
  waiting for transfers between devices  235 us (54%)
  blocking collectives  80.3 us (19%)
  local copies, waits for them, and re-layouts  55.1 us (13%)
  starting transfers between devices  21 us (5%)
  matrix products  14.5 us (3%)
  between operations  14.3 us (3%)
  other arithmetic  12.9 us (3%)
    all_to_all x1, waiting for transfers between devices, per_device(): lax.all_to_all(leaving, 'ep', split_axis=0, concat_axis=0, tiled=True)  130 us
    all_gather x1, waiting for transfers between devices, per_device(): lax.all_gather(product.reshape(count, hidden_width).astype(jnp.bfloat16),...  55.6 us
    all_to_all x1, blocking collectives, per_device(): lax.all_to_all(lax.all_to_all(result, 'dp', split_axis=0, concat_axis=1,...  48.3 us
    all_to_all x1, waiting for transfers between devices, per_device(): lax.all_to_all(outgoing, 'ep', split_axis=0, concat_axis=0, tiled=True)  24.9 us
    all_to_all x1, blocking collectives, per_device(): lax.all_to_all(result, 'dp', split_axis=0, concat_axis=1, tiled=True)  24.7 us
    all_to_all x1, waiting for transfers between devices, per_device(): lax.all_to_all(lax.all_to_all(outgoing, 'ep', split_axis=0, concat_axis=0...  16.8 us
    gather x1, local copies, waits for them, and re-layouts, per_device(): owned[jnp.maximum(wanted, 0)]  11.5 us
    gather x1, local copies, waits for them, and re-layouts, per_device(): arrived[cache_map.reshape(-1)]  11.4 us
  transfers between devices with their start and end apart: 5, of which 5 were waited for; matrix products, arithmetic and copies ran while one was open for 6% of the time, Pallas kernels for 0%

profile of v1, /device:TPU:0, one launch (start us, length us, event | category | flops | bytes accessed | tf_op | source)
XLA Modules:
  0.0 433.1 jit_solution(796962246271001310)
XLA Ops:
  7.2 0.0 copy-start
  7.2 0.0 copy-start.6
  7.2 1.1 fusion.14
  8.3 0.8 copy.46
  9.0 0.1 eq.36
  9.1 0.0 copy-done
  9.1 1.1 fusion.11
  10.3 0.3 select_reduce_fusion.1
  10.6 0.1 fusion.17
  10.7 0.2 reduce_window_sum.11
  10.9 0.2 select_reduce_fusion.3
  11.0 0.1 convert_element_type.96
  11.1 0.1 fusion.22
  11.2 0.2 select_reduce_fusion
  11.4 2.9 convolution_convert_fusion
  14.3 7.4 %all-to-all-start = ((bf16[16,16,3584]{2,1,0:T(8,128)(2,1)}), bf16[16,16,3584]{2,1,0:T(8,128)(2,1)S(1)}, u32[]{:S(2)}, u32[]{:S(2)}) async-start(bf16[16,16,3584]{2,1,0:T(8,128)(2,1)} %bitcast.45), calls=%async_computation | async-start | bytes 3670016 | tf_op jit(solution)/shard_map/all_to_all | solution.py:53
  21.7 0.0 copy-done.6
  21.8 11.5 %gather_fusion = bf16[224,128,128]{2,1,0:T(8,128)(2,1)} fusion(bf16[224,128,128]{2,1,0:T(8,128)(2,1)} %bitcast.46, s32[1024]{0:T(1024)S(1)} %pad_clamp_fusion.1), kind=kCustom, calls=%fused_computation | custom fusion | bytes 14680960 | tf_op jit(solution)/shard_map/gather | solution.py:46
  33.2 24.9 %all-to-all-done = bf16[16,16,3584]{2,1,0:T(8,128)(2,1)S(1)} async-done(((bf16[16,16,3584]{2,1,0:T(8,128)(2,1)}), bf16[16,16,3584]{2,1,0:T(8,128)(2,1)S(1)}, u32[]{:S(2)}, u32[]{:S(2)}) %all-to-all-start) | async-done | bytes 1835040 | tf_op jit(solution)/shard_map/all_to_all | solution.py:53
  58.1 1.5 all_to_all.57
  59.6 3.0 copy.49
  62.6 3.7 all-to-all-start.1
  66.3 6.6 %broadcast_select_fusion = bf16[224,128,128]{2,1,0:T(8,128)(2,1)} fusion(bf16[224,128,128]{2,1,0:T(8,128)(2,1)} %gather_fusion, pred[224]{0:T(512)(128)(4,1)S(1)} %compare_reduce_fusion), kind=kLoop, calls=%fused_computation.2 | loop fusion | flops 3670016 | bytes 14680288 | tf_op jit(solution)/shard_map/jit(_where)/select_n | solution.py:45
  73.0 0.0 copy-start.7
  73.0 16.8 %all-to-all-done.1 = bf16[256,2,1792]{2,0,1:T(8,128)(2,1)S(1)} async-done(((bf16[256,2,1792]{2,0,1:T(8,128)(2,1)}), bf16[256,2,1792]{2,0,1:T(8,128)(2,1)S(1)}, u32[]{:S(2)}, u32[]{:S(2)}) %all-to-all-start.1) | async-done | bytes 1835040 | tf_op jit(solution)/shard_map/all_to_all | solution.py:52
  89.7 9.6 %all-to-all-start.2 = ((bf16[224,128,128]{2,1,0:T(8,128)(2,1)}), bf16[224,128,128]{2,1,0:T(8,128)(2,1)}, u32[]{:S(2)}, u32[]{:S(2)}) async-start(bf16[224,128,128]{2,1,0:T(8,128)(2,1)} %broadcast_select_fusion), calls=%async_computation.2 | async-start | bytes 14680064 | tf_op jit(solution)/shard_map/all_to_all | solution.py:48
  99.4 0.2 all-gather.3.cloned.1.call-start
  99.6 0.0 copy-done.7
  99.6 2.4 reshape.181
  102.1 129.6 %all-to-all-done.2 = bf16[224,128,128]{2,1,0:T(8,128)(2,1)} async-done(((bf16[224,128,128]{2,1,0:T(8,128)(2,1)}), bf16[224,128,128]{2,1,0:T(8,128)(2,1)}, u32[]{:S(2)}, u32[]{:S(2)}) %all-to-all-start.2) | async-done | bytes 7340064 | tf_op jit(solution)/shard_map/all_to_all | solution.py:48
  231.7 11.4 %gather_fusion.1 = bf16[224,128,128]{2,1,0:T(8,128)(2,1)} fusion(bf16[224,128,128]{2,1,0:T(8,128)(2,1)} %all-to-all-done.2, s32[1024]{0:T(1024)S(1)} %pad_clamp_fusion), kind=kCustom, calls=%fused_computation.1 | custom fusion | bytes 14680960 | tf_op jit(solution)/shard_map/gather | solution.py:49
  243.1 9.4 %fusion.23 = (bf16[112,128,128]{2,1,0:T(8,128)(2,1)}, bf16[112,128,128]{2,1,0:T(8,128)(2,1)}) fusion(bf16[224,128,128]{2,1,0:T(8,128)(2,1)} %gather_fusion.1), kind=kLoop, calls=%fused_computation.53 | loop fusion | bytes 14680064 | tf_op jit(solution)/shard_map/slice | solution.py:51
  252.5 0.0 copy-start.2
  252.5 6.1 %copy.51 = bf16[14,8,128,128]{2,3,1,0:T(8,128)(2,1)} copy(bf16[14,8,128,128]{3,2,1,0:T(8,128)(2,1)} %bitcast.41) | data formatting | bytes 7340032 | tf_op jit(solution)/shard_map/squeeze | solution.py:50
  258.6 0.0 copy-done.2
  258.6 5.1 %bitcast_convert_fusion.1 = bf16[512,1024]{1,0:T(8,128)(2,1)} fusion(bf16[1024,14,128]{2,0,1:T(8,128)(2,1)} %bitcast.48, bf16[512,14,128]{2,1,0:T(8,128)(2,1)S(1)} %copy-done.2), kind=kOutput, calls=%fused_computation.13 | convolution fusion | flops 1879572480 | bytes 6553600 | tf_op jit(solution)/shard_map/nat,acts->ncs/dot_general | solution.py:61
  263.7 0.0 all-gather.3.cloned.1.call-update
  263.7 0.0 reduce-scatter.2.cloned.1.call-start
  263.8 4.3 %copy.54 = bf16[14,8,128,128]{3,2,0,1:T(8,128)(2,1)} copy(bf16[14,8,128,128]{3,2,1,0:T(8,128)(2,1)} %bitcast.40) | data formatting | bytes 7340032 | tf_op jit(solution)/shard_map/squeeze | solution.py:51
  268.1 55.6 %all-gather.3.cloned.1.call-done = bf16[1024,1024]{1,0:T(8,128)(2,1)} async-done(((bf16[512,1024]{1,0:T(8,128)(2,1)}), bf16[1024,1024]{1,0:T(8,128)(2,1)}) %all-gather.3.cloned.1.call-update) | async-done | bytes 2097168 | tf_op jit(solution)/shard_map/all_gather | solution.py:63
  323.7 2.2 reduce_sum.81
  325.9 0.6 fusion.4
  326.5 0.5 copy.53
  327.0 4.2 bitcast_convert_fusion
  331.2 24.7 %all_to_all.77 = bf16[2,256,1792]{2,1,0:T(8,128)(2,1)S(1)} all-to-all(bf16[2,256,1792]{2,1,0:T(8,128)(2,1)S(1)} %bitcast.50), channel_id=1, replica_groups=mesh['ep'=16,'dp'=2] {'dp'}, dimensions={0} | all-to-all | bytes 3670016 | tf_op jit(solution)/shard_map/all_to_all | solution.py:75
  355.9 1.9 copy.56
  357.7 0.0 copy-start.3
  357.8 0.0 copy-start.1
  357.8 2.2 all_to_all.64
  359.9 0.0 copy-start.5
  359.9 48.3 %all_to_all.78 = bf16[16,16,3584]{2,1,0:T(8,128)(2,1)S(1)} all-to-all(bf16[16,16,3584]{2,1,0:T(8,128)(2,1)} %all_to_all.64), channel_id=1, replica_groups=mesh['ep'=16,'dp'=2] {'ep'}, dimensions={0} | all-to-all | bytes 3670016 | tf_op jit(solution)/shard_map/all_to_all | solution.py:74
  408.3 0.0 copy-done.3
  408.3 0.5 fusion.12
  408.7 0.0 copy-start.4
  408.8 0.1 fusion.13
  408.9 7.3 %all_to_all.79 = bf16[16,2,1792]{2,0,1:T(8,128)(2,1)S(1)} all-to-all(bf16[16,2,1792]{2,0,1:T(8,128)(2,1)S(1)} %bitcast.53), channel_id=1, replica_groups=mesh['ep'=16,'dp'=2] {'dp'}, dimensions={1} | all-to-all | bytes 229376 | tf_op jit(solution)/shard_map/all_to_all | solution.py:86
  416.2 0.0 copy-done.5
  416.2 0.8 convolution_convert_fusion.1
  417.0 0.0 reduce-scatter.2.cloned.1.call-update
  417.0 8.0 %reduce-scatter.2.cloned.1.call-done = bf16[16,16]{1,0:T(8,128)(2,1)} async-done(((bf16[32,16]{1,0:T(8,128)(2,1)}), bf16[16,16]{1,0:T(8,128)(2,1)}) %reduce-scatter.2.cloned.1.call-update) | async-done | bytes 528 | tf_op jit(solution)/shard_map/reduce_scatter | solution.py:88
  425.0 1.3 add_divide_fusion
  426.3 0.0 copy-done.4
  426.3 0.0 copy-done.1
  (10 shorter events, 0.1 us)
Async XLA Ops:
  7.2 2.0 copy-start
  7.2 14.5 %copy-start.6 = (s32[1,224]{1,0:T(1,128)S(1)}, s32[1,224]{1,0:T(1,128)}, u32[]{:S(2)}) copy-start(s32[1,224]{1,0:T(1,128)} %param.14) | copy-start | bytes 2692
  14.3 43.8 %all-to-all-start = ((bf16[16,16,3584]{2,1,0:T(8,128)(2,1)}), bf16[16,16,3584]{2,1,0:T(8,128)(2,1)S(1)}, u32[]{:S(2)}, u32[]{:S(2)}) async-start(bf16[16,16,3584]{2,1,0:T(8,128)(2,1)} %bitcast.45), calls=%async_computation | async-start | bytes 3670016 | tf_op jit(solution)/shard_map/all_to_all | solution.py:53
  62.6 27.1 %all-to-all-start.1 = ((bf16[256,2,1792]{2,0,1:T(8,128)(2,1)}), bf16[256,2,1792]{2,0,1:T(8,128)(2,1)S(1)}, u32[]{:S(2)}, u32[]{:S(2)}) async-start(bf16[256,2,1792]{2,0,1:T(8,128)(2,1)} %copy.49), calls=%async_computation.1 | async-start | bytes 3670016 | tf_op jit(solution)/shard_map/all_to_all | solution.py:52
  73.0 26.7 %copy-start.7 = (s32[1,224]{1,0:T(1,128)S(1)}, s32[1,224]{1,0:T(1,128)}, u32[]{:S(2)}) copy-start(s32[1,224]{1,0:T(1,128)} %param.15) | copy-start | bytes 2692
  89.7 142.0 %all-to-all-start.2 = ((bf16[224,128,128]{2,1,0:T(8,128)(2,1)}), bf16[224,128,128]{2,1,0:T(8,128)(2,1)}, u32[]{:S(2)}, u32[]{:S(2)}) async-start(bf16[224,128,128]{2,1,0:T(8,128)(2,1)} %broadcast_select_fusion), calls=%async_computation.2 | async-start | bytes 14680064 | tf_op jit(solution)/shard_map/all_to_all | solution.py:48
  99.4 224.3 %all-gather.3.cloned.1.call-start = ((), (), s32[]{:S(2)}) async-start(), calls=%async_computation.8 | async-start | bytes 3145728 | tf_op jit(solution)/shard_map/all_gather | solution.py:63
  252.5 6.1 %copy-start.2 = (bf16[512,14,128]{2,1,0:T(8,128)(2,1)S(1)}, bf16[512,14,128]{2,1,0:T(8,128)(2,1)}, u32[]{:S(2)}) copy-start(bf16[512,14,128]{2,1,0:T(8,128)(2,1)} %reshape.181) | copy-start | bytes 5505028
  263.7 161.2 %reduce-scatter.2.cloned.1.call-start = ((), (), s32[]{:S(2)}) async-start(), calls=%async_computation.7 | async-start | bytes 12288 | tf_op jit(solution)/shard_map/reduce_scatter | solution.py:88
  357.7 50.5 %copy-start.3 = (bf16[16,3584]{1,0:T(8,128)(2,1)S(1)}, bf16[16,3584]{1,0:T(8,128)(2,1)}, u32[]{:S(2)}) copy-start(bf16[16,3584]{1,0:T(8,128)(2,1)} %param.8) | copy-start | bytes 344068
  357.8 68.5 %copy-start.1 = (bf16[3584,16]{0,1:T(8,128)(2,1)S(1)}, bf16[3584,16]{0,1:T(8,128)(2,1)}, u32[]{:S(2)}) copy-start(bf16[3584,16]{0,1:T(8,128)(2,1)} %param.10) | copy-start | bytes 344068
  359.9 56.3 %copy-start.5 = (bf16[1792,16]{0,1:T(8,128)(2,1)S(1)}, bf16[1792,16]{0,1:T(8,128)(2,1)}, u32[]{:S(2)}) copy-start(bf16[1792,16]{0,1:T(8,128)(2,1)} %param.11) | copy-start | bytes 172036
  408.7 17.5 %copy-start.4 = (bf16[16,3584]{1,0:T(8,128)(2,1)}, bf16[16,3584]{1,0:T(8,128)(2,1)S(1)}, u32[]{:S(2)}) copy-start(bf16[16,3584]{1,0:T(8,128)(2,1)S(1)} %get-tuple-element.9) | copy-start | bytes 344068
Sparse Core Ops, SparseCore 0:
  263.9 59.7 all-gather.2
  417.1 7.8 reduce-scatter.1
